TPU v7x, 128 devices: a whole 4x4x4 slice. The times are simulated.
128 devices in a mesh: wide: 32 (over y, z, core), narrow: 4 (over x).
Axes of the slice: x: 4, y: 4, z: 4, core: 2. Of those that a mesh axis runs over, the one named last changes fastest.
Arguments:
- object_field: float32 [2, 2048, 16384], P(None, 'narrow', 'wide')
- probe: float32 [4, 2, 256, 256], replicated, may hold values from -3 to 3
- patterns: float32 [4, 32, 6, 256, 256], P('narrow', 'wide'), may hold values from 0.1 to 4
- offsets: int32 [4, 32, 6, 2], P('narrow', 'wide'), may hold values from -128 to 384
- counts: int32 [4, 32], P('narrow', 'wide'), may hold values from 1 to 6
Outputs:
- object_new: float32 [2, 2048, 16384], P(None, 'narrow', 'wide')
- probe_new: float32 [4, 2, 256, 256], replicated
Inputs may be any that keep to these rules, and one draw needn't show every extreme that they name: A patch of 256 x 256 pixels at these offsets stays within the tile extended by 128 pixels on each side. `counts`: slots 0 to count - 1 of a tile are live, the others are ignored.
All inputs are finite; a program needn't handle non-finite values.
Results may differ from a plain program's by a relative error of at most 0.0003.
Values sent between devices are 32-bit elements; how exact they have to be, the bound alone decides.
A program may use at most 128 MiB of HBM per device.

v0:
```python
import jax
import jax.numpy as jnp
from jax import lax
from jax.sharding import PartitionSpec as P

H = 128
BATCHES = 3
POS = 2


def extended(shard, sides, width):
    for axis, dim in sides:
        size, length = (lax.axis_size(axis), shard.shape[dim])
        up = [(i, (i + 1) % size) for i in range(size - 1)]
        down = [(j, i) for i, j in up]
        last = lax.slice_in_dim(shard, length - width, length, axis=dim)
        leading = lax.slice_in_dim(shard, 0, width, axis=dim)
        before = lax.ppermute(last, axis, up)
        after = lax.ppermute(leading, axis, down)
        shard = jnp.concatenate([before, shard, after], axis=dim)
    return shard


def shifted(value, axis, steps):
    count = lax.axis_size(axis)
    leading, last = (max(0, -steps), min(count, count - steps))
    return lax.ppermute(value, axis, [(source, source + steps) for source in range(leading, last)])


def dft_tables(size):
    index = jnp.arange(size, dtype=jnp.int32)
    phase = index[:, None] * index[None, :] % size
    angle = -2.0 * jnp.pi * phase.astype(jnp.float32) / size
    scale = 1.0 / jnp.sqrt(jnp.float32(size))
    return (jnp.cos(angle) * scale, jnp.sin(angle) * scale)


def transform(real_part, imag_part, table_re, table_im):
    high = lax.Precision.HIGHEST
    left_re = jnp.einsum("jk,mkl->mjl", table_re, real_part, precision=high) - jnp.einsum(
        "jk,mkl->mjl", table_im, imag_part, precision=high
    )
    left_im = jnp.einsum("jk,mkl->mjl", table_re, imag_part, precision=high) + jnp.einsum(
        "jk,mkl->mjl", table_im, real_part, precision=high
    )
    out_re = jnp.einsum("mjk,kl->mjl", left_re, table_re, precision=high) - jnp.einsum(
        "mjk,kl->mjl", left_im, table_im, precision=high
    )
    out_im = jnp.einsum("mjk,kl->mjl", left_re, table_im, precision=high) + jnp.einsum(
        "mjk,kl->mjl", left_im, table_re, precision=high
    )
    return (out_re, out_im)


def slot_terms(patch, probe, measured, table_re, table_im):
    probe_re = probe[:, 0]
    probe_im = probe[:, 1]
    obj_re = patch[0]
    obj_im = patch[1]
    psi_re = probe_re * obj_re - probe_im * obj_im
    psi_im = probe_re * obj_im + probe_im * obj_re
    far_re, far_im = transform(psi_re, psi_im, table_re, table_im)
    intensity = jnp.sum(far_re * far_re + far_im * far_im, axis=0)
    keep = 1.0 - jnp.sqrt(measured) / jnp.sqrt(intensity + 0.1)
    back_re, back_im = transform(far_re * keep, far_im * keep, table_re, -table_im)
    grad_re = jnp.sum(probe_re * back_re + probe_im * back_im, axis=0)
    grad_im = jnp.sum(probe_re * back_im - probe_im * back_re, axis=0)
    pgrad_re = obj_re * back_re + obj_im * back_im
    pgrad_im = obj_re * back_im - obj_im * back_re
    square = jnp.sum(obj_re * obj_re + obj_im * obj_im)
    return (jnp.stack([grad_re, grad_im]), jnp.stack([pgrad_re, pgrad_im], axis=1), square)


def local(object_field, probe, patterns, offsets, counts):
    tile = object_field.shape[1]
    size = probe.shape[-1]
    table_re, table_im = dft_tables(size)
    padded = extended(object_field, (("wide", 2), ("narrow", 1)), H)
    gradient = jnp.zeros_like(padded)
    count_here = counts[0, 0]
    zero_at = jnp.zeros((), jnp.int32)
    for minibatch in range(BATCHES):
        probe_grad = jnp.zeros_like(probe)
        coverage = jnp.zeros((), jnp.float32)
        for position in range(POS):
            slot_at = minibatch * POS + position
            row_at = offsets[0, 0, slot_at, 0] + H
            col_at = offsets[0, 0, slot_at, 1] + H
            patch = lax.dynamic_slice(padded, (zero_at, row_at, col_at), (2, size, size))
            measured = patterns[0, 0, slot_at]

            def active(operands):
                return slot_terms(operands[0], operands[1], operands[2], table_re, table_im)

            def inactive(operands):
                return (
                    jnp.zeros((2, size, size), jnp.float32),
                    jnp.zeros_like(probe),
                    jnp.zeros((), jnp.float32),
                )

            obj_grad, pgrad, square = lax.cond(
                slot_at < count_here, active, inactive, (patch, probe, measured)
            )
            old = lax.dynamic_slice(gradient, (zero_at, row_at, col_at), (2, size, size))
            gradient = lax.dynamic_update_slice(gradient, old + obj_grad, (zero_at, row_at, col_at))
            probe_grad = probe_grad + pgrad
            coverage = coverage + square
        summed, total_cover = lax.psum((probe_grad, coverage), ("wide", "narrow"))
        probe = probe - summed / (total_cover / (size * size))
    left_part = gradient[:, :, :H]
    right_part = gradient[:, :, tile + H :]
    from_right = shifted(left_part, "wide", -1)
    from_left = shifted(right_part, "wide", 1)
    gradient = gradient.at[:, :, tile : tile + H].add(from_right)
    gradient = gradient.at[:, :, H : 2 * H].add(from_left)
    upper_part = gradient[:, :H, H : tile + H]
    lower_part = gradient[:, tile + H :, H : tile + H]
    from_below = shifted(upper_part, "narrow", -1)
    from_above = shifted(lower_part, "narrow", 1)
    core = gradient[:, H : tile + H, H : tile + H]
    core = core.at[:, tile - H :, :].add(from_below)
    core = core.at[:, :H, :].add(from_above)
    power = jnp.sum(probe[:, 0] ** 2 + probe[:, 1] ** 2, axis=0)
    top = jnp.max(power)
    return (object_field - 0.5 * core / top, probe)


def solution(mesh):
    placed = (
        P(None, "narrow", "wide"),
        P(),
        P("narrow", "wide", None, None, None),
        P("narrow", "wide", None, None),
        P("narrow", "wide"),
    )
    return jax.shard_map(
        local,
        mesh=mesh,
        in_specs=placed,
        out_specs=(P(None, "narrow", "wide"), P()),
        check_vma=False,
    )
```

profile of v0, /device:TPU:1, one launch (start us, length us, event | category | flops | bytes accessed | tf_op | source)
XLA Modules:
  0.0 804.1 jit_solution(2545430750540542145)
XLA Ops:
  8.6 4.9 collective-permute-start
  15.5 4.2 collective-permute-done
  19.9 4.2 collective-permute-done.1
  41.6 4.1 collective-permute-done.3
  45.7 4.6 pad_maximum_fusion.12
  50.3 37.6 %conditional.6 = (f32[2,256,256]{2,1,0:T(8,128)S(1)}, f32[]{:T(128)}, f32[4,2,256,256]{3,2,1,0:T(8,128)}) conditional(s32[]{:T(128)} %bitcast.174, () %tuple.80, (f32[4,2,256,256]{3,2,1,0:T(8,128)S(1)}, f32[2,768,768]{2,1,0:T(8,128)}, f32[256,256]{1,0:T(8,128)S(1)}, f32[256,256]{1,0:T(8,128)S(1)}, f32[256,256]{1,0:T(8,128)S(1)}, ...), branch_computations={%region_0.1_spmd, %region_1.6_spmd.clone} | conditional | flops 12897091584 | bytes 71303224 | solution.py:102
  87.9 38.3 %conditional.7 = (f32[2,256,256]{2,1,0:T(8,128)S(1)}, f32[]{:T(128)}, f32[4,2,256,256]{3,2,1,0:T(8,128)}) conditional(s32[]{:T(128)} %bitcast.183, () %tuple.82, (f32[4,2,256,256]{3,2,1,0:T(8,128)S(1)}, f32[2,768,768]{2,1,0:T(8,128)}, f32[256,256]{1,0:T(8,128)S(1)}, f32[256,256]{1,0:T(8,128)S(1)}, f32[256,256]{1,0:T(8,128)S(1)}, ...), branch_computations={%region_6.7_spmd, %region_7.12_spmd.clone} | conditional | flops 12897091584 | bytes 71303224 | solution.py:102
  135.5 71.5 %psum.43 = f32[]{:T(128)} all-reduce(f32[]{:T(128)S(6)} %add.746), channel_id=1, replica_groups=mesh['wide'=32,'narrow'=4] {'wide','narrow'}, use_global_device_ids=true, to_apply=%region_13.14 | all-reduce | flops 1 | bytes 8 | tf_op jit(solution)/shard_map/psum | solution.py:109
  207.7 80.3 %all-reduce.4.cloned.1.call-done = f32[4,2,256,256]{3,2,1,0:T(8,128)} async-done(((f32[4,2,256,256]{3,2,1,0:T(8,128)}), f32[4,2,256,256]{3,2,1,0:T(8,128)}) %all-reduce.4.cloned.1.call-update) | async-done | bytes 2097168 | tf_op jit(solution)/shard_map/psum | solution.py:109
  290.6 37.3 %conditional.8 = (f32[2,256,256]{2,1,0:T(8,128)}, f32[]{:T(128)}, f32[4,2,256,256]{3,2,1,0:T(8,128)}) conditional(s32[]{:T(128)} %bitcast.188, () %tuple.84, (f32[4,2,256,256]{3,2,1,0:T(8,128)S(1)}, f32[2,768,768]{2,1,0:T(8,128)}, s32[]{:T(128)}, s32[]{:T(128)}, f32[256,256]{1,0:T(8,128)S(1)}, /*index=5*/f32[256,256]{1,0:T(8,128)S(1)}, ...), branch_computations={%region_14.15_spmd, %region_15.20_spmd} | conditional | flops 12897091584 | bytes 71303224 | solution.py:102
  327.9 12.4 %conditional.9 = (f32[2,256,256]{2,1,0:T(8,128)}, f32[]{:T(128)}, f32[4,2,256,256]{3,2,1,0:T(8,128)}) conditional(s32[]{:T(128)} %bitcast.193, () %tuple.86, (f32[4,2,256,256]{3,2,1,0:T(8,128)S(1)}, f32[2,768,768]{2,1,0:T(8,128)}, s32[]{:T(128)}, s32[]{:T(128)}, f32[256,256]{1,0:T(8,128)S(1)}, /*index=5*/f32[256,256]{1,0:T(8,128)S(1)}, ...), branch_computations={%region_20.21_spmd, %region_21.26_spmd} | conditional | flops 12897091584 | bytes 71303224 | solution.py:102
  351.4 6.5 dynamic_update_slice.18
  359.4 6.6 dynamic_update_slice.19
  366.1 89.8 %psum.45 = f32[]{:T(128)} all-reduce(f32[]{:T(128)S(6)} %add.766), channel_id=1, replica_groups=mesh['wide'=32,'narrow'=4] {'wide','narrow'}, use_global_device_ids=true, to_apply=%region_27.28 | all-reduce | flops 1 | bytes 8 | tf_op jit(solution)/shard_map/psum | solution.py:109
  458.1 6.4 dynamic_update_slice.20
  466.0 6.6 dynamic_update_slice.21
  472.6 45.5 %all-reduce.6.cloned.1.call-done = f32[4,2,256,256]{3,2,1,0:T(8,128)} async-done(((f32[4,2,256,256]{3,2,1,0:T(8,128)}), f32[4,2,256,256]{3,2,1,0:T(8,128)}) %all-reduce.6.cloned.1.call-update) | async-done | bytes 2097168 | tf_op jit(solution)/shard_map/psum | solution.py:109
  521.3 11.7 %conditional.10 = (f32[2,256,256]{2,1,0:T(8,128)}, f32[]{:T(128)}, f32[4,2,256,256]{3,2,1,0:T(8,128)}) conditional(s32[]{:T(128)} %bitcast.198, () %tuple.88, (f32[4,2,256,256]{3,2,1,0:T(8,128)}, f32[2,768,768]{2,1,0:T(8,128)}, s32[]{:T(128)}, s32[]{:T(128)}, f32[256,256]{1,0:T(8,128)S(1)}, /*index=5*/f32[256,256]{1,0:T(8,128)S(1)}, ...), branch_computations={%region_28.29_spmd, %region_29.34_spmd} | conditional | flops 12897091584 | bytes 79691856 | solution.py:102
  534.6 6.8 dynamic_update_slice.22
  541.4 5.4 conditional.11
  548.2 6.9 dynamic_update_slice.23
  556.3 60.8 %collective-permute-start.4 = (f32[2,768,128]{2,1,0:T(8,128)S(1)}, f32[2,768,128]{2,1,0:T(8,128)S(1)}, u32[]{:S(2)}, u32[]{:S(2)}) collective-permute-start(f32[2,768,128]{2,1,0:T(8,128)S(1)} %slice.336), channel_id=1, source_target_pairs={{4,0},{8,4},{12,8},{16,12},{20,16},{24,20},{28,24},{32,28},{36,32}... | collective-permute-start | bytes 2359304 | tf_op jit(solution)/shard_map/ppermute | solution.py:27
  627.5 75.8 %psum.47 = f32[]{:T(128)} all-reduce(f32[]{:T(128)S(6)} %add.782), channel_id=1, replica_groups=mesh['wide'=32,'narrow'=4] {'wide','narrow'}, use_global_device_ids=true, to_apply=%region_41.42 | all-reduce | flops 1 | bytes 8 | tf_op jit(solution)/shard_map/psum | solution.py:109
  711.0 76.2 %all-reduce.8.cloned.1.call-done = f32[4,2,256,256]{3,2,1,0:T(8,128)} async-done(((f32[4,2,256,256]{3,2,1,0:T(8,128)}), f32[4,2,256,256]{3,2,1,0:T(8,128)}) %all-reduce.8.cloned.1.call-update) | async-done | bytes 2097168 | tf_op jit(solution)/shard_map/psum | solution.py:109
  (131 shorter events, 180.5 us)
Async XLA Ops:
  7.2 12.6 %copy-start.3 = (f32[2,512,512]{2,1,0:T(8,128)S(1)}, f32[2,512,512]{2,1,0:T(8,128)}, u32[]{:S(2)}) copy-start(f32[2,512,512]{2,1,0:T(8,128)} %param.25) | copy-start | bytes 6291460
  7.2 280.9 %all-reduce.4.cloned.1.call-start = ((), (), s32[]{:S(2)}) async-start(), calls=%async_computation | async-start | bytes 4194304 | tf_op jit(solution)/shard_map/psum | solution.py:109
  8.6 11.0 %collective-permute-start = (f32[2,512,128]{2,1,0:T(8,128)S(1)}, f32[2,512,128]{2,1,0:T(8,128)S(1)}, u32[]{:S(2)}, u32[]{:S(2)}) collective-permute-start(f32[2,512,128]{2,1,0:T(8,128)S(1)} %get-tuple-element.871), channel_id=1, source_target_pairs={{0,4},{4,8},{8,12},{12,16},{16,20},{20,24},{24,28},{28,32},{32,36}... | collective-permute-start | bytes 1572872 | tf_op jit(solution)/shard_map/ppermute | solution.py:18
  13.6 10.5 %collective-permute-start.1 = (f32[2,512,128]{2,1,0:T(8,128)S(1)}, f32[2,512,128]{2,1,0:T(8,128)S(1)}, u32[]{:S(2)}, u32[]{:S(2)}) collective-permute-start(f32[2,512,128]{2,1,0:T(8,128)S(1)} %get-tuple-element.870), channel_id=1, source_target_pairs={{4,0},{8,4},{12,8},{16,12},{20,16},{24,20},{28,24},{32,28},{36,32}... | collective-permute-start | bytes 1572872 | tf_op jit(solution)/shard_map/ppermute | solution.py:19
  19.9 11.6 %copy-start.8 = (s32[1,1,6,2]{2,3,1,0:T(2,128)S(1)}, s32[1,1,6,2]{2,3,1,0:T(2,128)}, u32[]{:S(2)}) copy-start(s32[1,1,6,2]{2,3,1,0:T(2,128)} %param.28) | copy-start | bytes 148
  24.1 1.7 copy-start.5
  27.1 14.5 %collective-permute-start.2 = (f32[2,128,768]{2,1,0:T(8,128)}, f32[2,128,768]{2,1,0:T(8,128)S(1)}, u32[]{:S(2)}, u32[]{:S(2)}) collective-permute-start(f32[2,128,768]{2,1,0:T(8,128)} %get-tuple-element.868), channel_id=1, source_target_pairs={{0,1},{1,2},{2,3},{4,5},{5,6},{6,7},{8,9},{9,10},{10,11},{12,13},{... | collective-permute-start | bytes 2359304 | tf_op jit(solution)/shard_map/ppermute | solution.py:18
  30.2 15.5 %collective-permute-start.3 = (f32[2,128,768]{2,1,0:T(8,128)}, f32[2,128,768]{2,1,0:T(8,128)}, u32[]{:S(2)}, u32[]{:S(2)}) collective-permute-start(f32[2,128,768]{2,1,0:T(8,128)} %get-tuple-element.869), channel_id=1, source_target_pairs={{1,0},{2,1},{3,2},{5,4},{6,5},{7,6},{9,8},{10,9},{11,10},{13,12},{... | collective-permute-start | bytes 2359304 | tf_op jit(solution)/shard_map/ppermute | solution.py:19
  38.9 11.4 %copy-start.2 = (f32[4,2,256,256]{3,2,1,0:T(8,128)S(1)}, f32[4,2,256,256]{3,2,1,0:T(8,128)}, u32[]{:S(2)}) copy-start(f32[4,2,256,256]{3,2,1,0:T(8,128)} %param.26) | copy-start | bytes 6291460
  126.2 4.0 copy-start.7
  130.3 387.8 %all-reduce.6.cloned.1.call-start = ((), (), s32[]{:S(2)}) async-start(), calls=%async_computation.1 | async-start | bytes 4194304 | tf_op jit(solution)/shard_map/psum | solution.py:109
  344.1 443.1 %all-reduce.8.cloned.1.call-start = ((), (), s32[]{:S(2)}) async-start(), calls=%async_computation.2 | async-start | bytes 4194304 | tf_op jit(solution)/shard_map/psum | solution.py:109
  532.9 8.5 %copy-start = (f32[4,2,256,256]{3,2,1,0:T(8,128)S(1)}, f32[4,2,256,256]{3,2,1,0:T(8,128)}, u32[]{:S(2)}) copy-start(f32[4,2,256,256]{3,2,1,0:T(8,128)} %divide_subtract_fusion.2) | copy-start | bytes 6291460
  556.3 62.7 %collective-permute-start.4 = (f32[2,768,128]{2,1,0:T(8,128)S(1)}, f32[2,768,128]{2,1,0:T(8,128)S(1)}, u32[]{:S(2)}, u32[]{:S(2)}) collective-permute-start(f32[2,768,128]{2,1,0:T(8,128)S(1)} %slice.336), channel_id=1, source_target_pairs={{4,0},{8,4},{12,8},{16,12},{20,16},{24,20},{28,24},{32,28},{36,32}... | collective-permute-start | bytes 2359304 | tf_op jit(solution)/shard_map/ppermute | solution.py:27
  621.8 82.2 %collective-permute-start.5 = (f32[2,768,128]{2,1,0:T(8,128)}, f32[2,768,128]{2,1,0:T(8,128)S(1)}, u32[]{:S(2)}, u32[]{:S(2)}) collective-permute-start(f32[2,768,128]{2,1,0:T(8,128)} %get-tuple-element.866), channel_id=1, source_target_pairs={{0,4},{4,8},{8,12},{12,16},{16,20},{20,24},{24,28},{28,32},{32,36}... | collective-permute-start | bytes 2359304 | tf_op jit(solution)/shard_map/ppermute | solution.py:27
  708.4 86.1 %collective-permute-start.7 = (f32[2,128,512]{2,1,0:T(8,128)}, f32[2,128,512]{2,1,0:T(8,128)S(1)}, u32[]{:S(2)}, u32[]{:S(2)}) collective-permute-start(f32[2,128,512]{2,1,0:T(8,128)} %get-tuple-element.864), channel_id=1, source_target_pairs={{0,1},{1,2},{2,3},{4,5},{5,6},{6,7},{8,9},{9,10},{10,11},{12,13},{... | collective-permute-start | bytes 1572872 | tf_op jit(solution)/shard_map/ppermute | solution.py:27
  709.7 83.3 %collective-permute-start.6 = (f32[2,128,512]{2,1,0:T(8,128)}, f32[2,128,512]{2,1,0:T(8,128)}, u32[]{:S(2)}, u32[]{:S(2)}) collective-permute-start(f32[2,128,512]{2,1,0:T(8,128)} %get-tuple-element.865), channel_id=1, source_target_pairs={{1,0},{2,1},{3,2},{5,4},{6,5},{7,6},{9,8},{10,9},{11,10},{13,12},{... | collective-permute-start | bytes 1572872 | tf_op jit(solution)/shard_map/ppermute | solution.py:27
  789.1 1.3 copy-start.6
  793.0 1.9 copy-start.4
Sparse Core Ops, SparseCore 0:
  130.4 157.6 all-reduce.3
  344.3 173.7 all-reduce.5
  627.6 159.5 all-reduce.7
where the time goes:
time: 809 us; the launch traced here: 804 us
  blocking collectives  237 us (29%)
  waiting for transfers between devices  219 us (27%)
  matrix products  91.7 us (11%)
  starting transfers between devices  76.8 us (9%)
  local copies, waits for them, and re-layouts  65 us (8%)
  other arithmetic  52.5 us (6%)
  between operations  31.9 us (4%)
  loops' own time  29.9 us (4%)
    psum x3, blocking collectives, local(): summed, total_cover = lax.psum((probe_grad, coverage), ('wide', 'narrow'))  237 us
    psum x3, waiting for transfers between devices, local(): summed, total_cover = lax.psum((probe_grad, coverage), ('wide', 'narrow'))  202 us
    ppermute x4, starting transfers between devices, shifted(): lax.ppermute(value, axis, [(source, source + steps) for source in range(l...  65.4 us
    dynamic_update_slice x6, local copies, waits for them, and re-layouts, local(): lax.dynamic_update_slice(gradient, old + obj_grad, (zero_at, row_at, col_...  39.8 us
    another operation x6, loops' own time, local(): lax.cond(slot_at < count_here, active, inactive, (patch, probe, measured))  29.9 us
  transfers between devices with their start and end apart: 11, of which 8 were waited for; matrix products, arithmetic and copies ran while one was open for 6% of the time, Pallas kernels for 0%

commit v1 on v0

--- a/solution.py
+++ b/solution.py
@@ -6,6 +6,9 @@
 H = 128
 BATCHES = 3
 POS = 2
+supply_all_yards_here = lambda mat, mesh_name, peer_axis: lax.psum(
+    lax.psum(mat, mesh_name), peer_axis
+)
 
 
 def extended(shard, sides, width):
@@ -106,7 +109,7 @@
             gradient = lax.dynamic_update_slice(gradient, old + obj_grad, (zero_at, row_at, col_at))
             probe_grad = probe_grad + pgrad
             coverage = coverage + square
-        summed, total_cover = lax.psum((probe_grad, coverage), ("wide", "narrow"))
+        summed, total_cover = supply_all_yards_here((probe_grad, coverage), "wide", "narrow")
         probe = probe - summed / (total_cover / (size * size))
     left_part = gradient[:, :, :H]
     right_part = gradient[:, :, tile + H :]

time: 809 us -> 945 us (1.17)
  waiting for transfers between devices: 219 us -> 359 us
  blocking collectives: 237 us -> 216 us
    psum x3 -> x6, waiting for transfers between devices: 202 us -> 343 us  [the longest x3 343 us: lax.psum(mat, mesh_name)]
    psum x3 -> x6, blocking collectives: 237 us -> 216 us  [the longest x3 190 us: lax.psum(mat, mesh_name)]
  transfers between devices with their start and end apart: 11 -> 14, of which waited for: 8 -> 7; matrix products, arithmetic and copies ran while one was open for 6% -> 6% of each run, Pallas kernels for 0% -> 0%
where the time goes in v1:
time: 945 us; the launch traced here: 935 us
  waiting for transfers between devices  359 us (38%)
  blocking collectives  216 us (23%)
  matrix products  91.7 us (10%)
  starting transfers between devices  85.4 us (9%)
  local copies, waits for them, and re-layouts  66.7 us (7%)
  other arithmetic  57.5 us (6%)
  between operations  32 us (3%)
  loops' own time  27.3 us (3%)
    psum x3, waiting for transfers between devices, lax.psum(mat, mesh_name)  343 us
    psum x3, blocking collectives, lax.psum(mat, mesh_name)  190 us
    ppermute x4, starting transfers between devices, shifted(): lax.ppermute(value, axis, [(source, source + steps) for source in range(l...  73.9 us
    dynamic_update_slice x6, local copies, waits for them, and re-layouts, local(): lax.dynamic_update_slice(gradient, old + obj_grad, (zero_at, row_at, col_...  39.8 us
    another operation x6, loops' own time, local(): lax.cond(slot_at < count_here, active, inactive, (patch, probe, measured))  27.3 us
    psum x3, blocking collectives, lax.psum(lax.psum(mat, mesh_name), peer_axis)  26.1 us
  transfers between devices with their start and end apart: 14, of which 7 were waited for; matrix products, arithmetic and copies ran while one was open for 6% of the time, Pallas kernels for 0%

profile of v1, /device:TPU:1, one launch (start us, length us, event | category | flops | bytes accessed | tf_op | source)
XLA Modules:
  0.0 935.2 jit_solution(13289251375042594683)
XLA Ops:
  8.6 4.9 collective-permute-start
  45.7 4.6 pad_maximum_fusion.12
  50.3 37.7 %conditional.6 = (f32[2,256,256]{2,1,0:T(8,128)S(1)}, f32[]{:T(128)}, f32[4,2,256,256]{3,2,1,0:T(8,128)}) conditional(s32[]{:T(128)} %bitcast.174, () %tuple.80, (f32[4,2,256,256]{3,2,1,0:T(8,128)S(1)}, f32[2,768,768]{2,1,0:T(8,128)}, f32[256,256]{1,0:T(8,128)S(1)}, f32[256,256]{1,0:T(8,128)S(1)}, f32[256,256]{1,0:T(8,128)S(1)}, ...), branch_computations={%region_0.1_spmd, %region_1.6_spmd.clone} | conditional | flops 12897091584 | bytes 71303224 | solution.py:105
  88.0 37.8 %conditional.7 = (f32[2,256,256]{2,1,0:T(8,128)}, f32[]{:T(128)}, f32[4,2,256,256]{3,2,1,0:T(8,128)}) conditional(s32[]{:T(128)} %bitcast.183, () %tuple.82, (f32[4,2,256,256]{3,2,1,0:T(8,128)S(1)}, f32[2,768,768]{2,1,0:T(8,128)}, f32[256,256]{1,0:T(8,128)S(1)}, f32[256,256]{1,0:T(8,128)S(1)}, f32[256,256]{1,0:T(8,128)S(1)}, ...), branch_computations={%region_6.7_spmd, %region_7.12_spmd.clone} | conditional | flops 12897091584 | bytes 71303224 | solution.py:105
  129.7 114.4 %all-reduce.7.cloned.1.call-done = f32[4,2,256,256]{3,2,1,0:T(8,128)} async-done(((f32[4,2,256,256]{3,2,1,0:T(8,128)}), f32[4,2,256,256]{3,2,1,0:T(8,128)}) %all-reduce.7.cloned.1.call-update) | async-done | bytes 2097168 | tf_op jit(solution)/shard_map/psum | solution.py:10
  249.0 63.1 %psum.86 = f32[]{:T(128)} all-reduce(f32[]{:T(128)S(6)} %add.758), channel_id=1, replica_groups=mesh['wide'=32,'narrow'=4] {'wide'}, use_global_device_ids=true, to_apply=%region_14.15 | all-reduce | flops 1 | bytes 8 | tf_op jit(solution)/shard_map/psum | solution.py:10
  312.1 9.0 psum.87
  324.4 37.1 %conditional.8 = (f32[2,256,256]{2,1,0:T(8,128)}, f32[]{:T(128)}, f32[4,2,256,256]{3,2,1,0:T(8,128)}) conditional(s32[]{:T(128)} %bitcast.188, () %tuple.84, (f32[4,2,256,256]{3,2,1,0:T(8,128)S(1)}, f32[2,768,768]{2,1,0:T(8,128)}, s32[]{:T(128)}, s32[]{:T(128)}, f32[256,256]{1,0:T(8,128)S(1)}, /*index=5*/f32[256,256]{1,0:T(8,128)S(1)}, ...), branch_computations={%region_16.17_spmd, %region_17.22_spmd} | conditional | flops 12897091584 | bytes 71303224 | solution.py:105
  361.5 11.8 %conditional.9 = (f32[2,256,256]{2,1,0:T(8,128)}, f32[]{:T(128)}, f32[4,2,256,256]{3,2,1,0:T(8,128)}) conditional(s32[]{:T(128)} %bitcast.193, () %tuple.86, (f32[4,2,256,256]{3,2,1,0:T(8,128)S(1)}, f32[2,768,768]{2,1,0:T(8,128)}, s32[]{:T(128)}, s32[]{:T(128)}, f32[256,256]{1,0:T(8,128)S(1)}, /*index=5*/f32[256,256]{1,0:T(8,128)S(1)}, ...), branch_computations={%region_22.23_spmd, %region_23.28_spmd} | conditional | flops 12897091584 | bytes 71303224 | solution.py:105
  377.3 132.3 %all-reduce.11.cloned.1.call-done = f32[4,2,256,256]{3,2,1,0:T(8,128)} async-done(((f32[4,2,256,256]{3,2,1,0:T(8,128)}), f32[4,2,256,256]{3,2,1,0:T(8,128)}) %all-reduce.11.cloned.1.call-update) | async-done | bytes 2097168 | tf_op jit(solution)/shard_map/psum | solution.py:10
  517.1 6.5 dynamic_update_slice.18
  525.1 63.1 %psum.90 = f32[]{:T(128)} all-reduce(f32[]{:T(128)S(6)} %add.778), channel_id=1, replica_groups=mesh['wide'=32,'narrow'=4] {'wide'}, use_global_device_ids=true, to_apply=%region_30.31 | all-reduce | flops 1 | bytes 8 | tf_op jit(solution)/shard_map/psum | solution.py:10
  588.3 6.6 dynamic_update_slice.19
  594.9 9.3 psum.91
  606.3 6.4 dynamic_update_slice.20
  614.3 6.6 dynamic_update_slice.21
  624.0 11.7 %conditional.10 = (f32[2,256,256]{2,1,0:T(8,128)}, f32[]{:T(128)}, f32[4,2,256,256]{3,2,1,0:T(8,128)}) conditional(s32[]{:T(128)} %bitcast.198, () %tuple.88, (f32[4,2,256,256]{3,2,1,0:T(8,128)}, f32[2,768,768]{2,1,0:T(8,128)}, s32[]{:T(128)}, s32[]{:T(128)}, f32[256,256]{1,0:T(8,128)S(1)}, /*index=5*/f32[256,256]{1,0:T(8,128)S(1)}, ...), branch_computations={%region_32.33_spmd, %region_33.38_spmd} | conditional | flops 12897091584 | bytes 79691856 | solution.py:105
  637.4 6.8 dynamic_update_slice.22
  644.2 4.8 conditional.11
  650.4 6.9 dynamic_update_slice.23
  658.4 66.7 %collective-permute-start.4 = (f32[2,768,128]{2,1,0:T(8,128)S(1)}, f32[2,768,128]{2,1,0:T(8,128)}, u32[]{:S(2)}, u32[]{:S(2)}) collective-permute-start(f32[2,768,128]{2,1,0:T(8,128)S(1)} %slice.336), channel_id=1, source_target_pairs={{4,0},{8,4},{12,8},{16,12},{20,16},{24,20},{28,24},{32,28},{36,32}... | collective-permute-start | bytes 2359304 | tf_op jit(solution)/shard_map/ppermute | solution.py:30
  734.0 96.4 %all-reduce.15.cloned.1.call-done = f32[4,2,256,256]{3,2,1,0:T(8,128)} async-done(((f32[4,2,256,256]{3,2,1,0:T(8,128)}), f32[4,2,256,256]{3,2,1,0:T(8,128)}) %all-reduce.15.cloned.1.call-update) | async-done | bytes 2097168 | tf_op jit(solution)/shard_map/psum | solution.py:10
  840.2 63.7 %psum.94 = f32[]{:T(128)} all-reduce(f32[]{:T(128)S(6)} %add.794), channel_id=1, replica_groups=mesh['wide'=32,'narrow'=4] {'wide'}, use_global_device_ids=true, to_apply=%region_46.47 | all-reduce | flops 1 | bytes 8 | tf_op jit(solution)/shard_map/psum | solution.py:10
  903.9 7.8 psum.95
  (141 shorter events, 200.8 us)
Async XLA Ops:
  7.2 12.6 %copy-start.3 = (f32[2,512,512]{2,1,0:T(8,128)S(1)}, f32[2,512,512]{2,1,0:T(8,128)}, u32[]{:S(2)}) copy-start(f32[2,512,512]{2,1,0:T(8,128)} %param.25) | copy-start | bytes 6291460
  7.2 236.9 %all-reduce.7.cloned.1.call-start = ((), (), s32[]{:S(2)}) async-start(), calls=%async_computation | async-start | bytes 4194304 | tf_op jit(solution)/shard_map/psum | solution.py:10
  8.6 11.0 %collective-permute-start = (f32[2,512,128]{2,1,0:T(8,128)S(1)}, f32[2,512,128]{2,1,0:T(8,128)S(1)}, u32[]{:S(2)}, u32[]{:S(2)}) collective-permute-start(f32[2,512,128]{2,1,0:T(8,128)S(1)} %get-tuple-element.871), channel_id=1, source_target_pairs={{0,4},{4,8},{8,12},{12,16},{16,20},{20,24},{24,28},{28,32},{32,36}... | collective-permute-start | bytes 1572872 | tf_op jit(solution)/shard_map/ppermute | solution.py:21
  13.6 10.5 %collective-permute-start.1 = (f32[2,512,128]{2,1,0:T(8,128)S(1)}, f32[2,512,128]{2,1,0:T(8,128)S(1)}, u32[]{:S(2)}, u32[]{:S(2)}) collective-permute-start(f32[2,512,128]{2,1,0:T(8,128)S(1)} %get-tuple-element.870), channel_id=1, source_target_pairs={{4,0},{8,4},{12,8},{16,12},{20,16},{24,20},{28,24},{32,28},{36,32}... | collective-permute-start | bytes 1572872 | tf_op jit(solution)/shard_map/ppermute | solution.py:22
  19.9 11.6 %copy-start.7 = (s32[1,1,6,2]{2,3,1,0:T(2,128)S(1)}, s32[1,1,6,2]{2,3,1,0:T(2,128)}, u32[]{:S(2)}) copy-start(s32[1,1,6,2]{2,3,1,0:T(2,128)} %param.28) | copy-start | bytes 148
  24.1 1.7 copy-start.5
  27.1 14.5 %collective-permute-start.2 = (f32[2,128,768]{2,1,0:T(8,128)}, f32[2,128,768]{2,1,0:T(8,128)S(1)}, u32[]{:S(2)}, u32[]{:S(2)}) collective-permute-start(f32[2,128,768]{2,1,0:T(8,128)} %get-tuple-element.868), channel_id=1, source_target_pairs={{0,1},{1,2},{2,3},{4,5},{5,6},{6,7},{8,9},{9,10},{10,11},{12,13},{... | collective-permute-start | bytes 2359304 | tf_op jit(solution)/shard_map/ppermute | solution.py:21
  30.2 15.5 %collective-permute-start.3 = (f32[2,128,768]{2,1,0:T(8,128)}, f32[2,128,768]{2,1,0:T(8,128)}, u32[]{:S(2)}, u32[]{:S(2)}) collective-permute-start(f32[2,128,768]{2,1,0:T(8,128)} %get-tuple-element.869), channel_id=1, source_target_pairs={{1,0},{2,1},{3,2},{5,4},{6,5},{7,6},{9,8},{10,9},{11,10},{13,12},{... | collective-permute-start | bytes 2359304 | tf_op jit(solution)/shard_map/ppermute | solution.py:22
  38.8 11.5 %copy-start.2 = (f32[4,2,256,256]{3,2,1,0:T(8,128)S(1)}, f32[4,2,256,256]{3,2,1,0:T(8,128)}, u32[]{:S(2)}) copy-start(f32[4,2,256,256]{3,2,1,0:T(8,128)} %param.26) | copy-start | bytes 6291460
  129.6 192.2 %all-reduce.9.cloned.1.call-start = ((), (), s32[]{:S(2)}) async-start(), calls=%async_computation.1 | async-start | bytes 4194304 | tf_op jit(solution)/shard_map/psum | solution.py:9
  244.1 265.5 %all-reduce.11.cloned.1.call-start = ((), (), s32[]{:S(2)}) async-start(), calls=%async_computation.2 | async-start | bytes 4194304 | tf_op jit(solution)/shard_map/psum | solution.py:10
  377.2 243.6 %all-reduce.13.cloned.1.call-start = ((), (), s32[]{:S(2)}) async-start(), calls=%async_computation.3 | async-start | bytes 4194304 | tf_op jit(solution)/shard_map/psum | solution.py:9
  509.6 320.8 %all-reduce.15.cloned.1.call-start = ((), (), s32[]{:S(2)}) async-start(), calls=%async_computation.4 | async-start | bytes 4194304 | tf_op jit(solution)/shard_map/psum | solution.py:10
  635.7 8.5 copy-start
  658.4 70.6 %collective-permute-start.4 = (f32[2,768,128]{2,1,0:T(8,128)S(1)}, f32[2,768,128]{2,1,0:T(8,128)}, u32[]{:S(2)}, u32[]{:S(2)}) collective-permute-start(f32[2,768,128]{2,1,0:T(8,128)S(1)} %slice.336), channel_id=1, source_target_pairs={{4,0},{8,4},{12,8},{16,12},{20,16},{24,20},{28,24},{32,28},{36,32}... | collective-permute-start | bytes 2359304 | tf_op jit(solution)/shard_map/ppermute | solution.py:30
  729.0 190.3 %all-reduce.17.cloned.1.call-start = ((), (), s32[]{:S(2)}) async-start(), calls=%async_computation.5 | async-start | bytes 4194304 | tf_op jit(solution)/shard_map/psum | solution.py:9
  732.1 98.4 %collective-permute-start.5 = (f32[2,768,128]{2,1,0:T(8,128)}, f32[2,768,128]{2,1,0:T(8,128)S(1)}, u32[]{:S(2)}, u32[]{:S(2)}) collective-permute-start(f32[2,768,128]{2,1,0:T(8,128)} %get-tuple-element.866), channel_id=1, source_target_pairs={{0,4},{4,8},{8,12},{12,16},{16,20},{20,24},{24,28},{28,32},{32,36}... | collective-permute-start | bytes 2359304 | tf_op jit(solution)/shard_map/ppermute | solution.py:30
  834.9 80.5 %collective-permute-start.6 = (f32[2,128,512]{2,1,0:T(8,128)}, f32[2,128,512]{2,1,0:T(8,128)S(1)}, u32[]{:S(2)}, u32[]{:S(2)}) collective-permute-start(f32[2,128,512]{2,1,0:T(8,128)} %get-tuple-element.865), channel_id=1, source_target_pairs={{1,0},{2,1},{3,2},{5,4},{6,5},{7,6},{9,8},{10,9},{11,10},{13,12},{... | collective-permute-start | bytes 1572872 | tf_op jit(solution)/shard_map/ppermute | solution.py:30
  836.2 81.2 %collective-permute-start.7 = (f32[2,128,512]{2,1,0:T(8,128)}, f32[2,128,512]{2,1,0:T(8,128)S(1)}, u32[]{:S(2)}, u32[]{:S(2)}) collective-permute-start(f32[2,128,512]{2,1,0:T(8,128)} %get-tuple-element.864), channel_id=1, source_target_pairs={{0,1},{1,2},{2,3},{4,5},{5,6},{6,7},{8,9},{9,10},{10,11},{12,13},{... | collective-permute-start | bytes 1572872 | tf_op jit(solution)/shard_map/ppermute | solution.py:30
  921.1 1.3 copy-start.6
  922.4 1.6 copy-start.4
Sparse Core Ops, SparseCore 0:
  129.7 114.2 all-reduce.6
  246.4 57.9 all-reduce.8
  377.3 132.2 all-reduce.10
  511.8 58.0 all-reduce.12
  729.1 101.2 all-reduce.14
  832.7 67.4 all-reduce.16
